TPU v7x, 32 devices: a whole 2x2x4 slice. The times are simulated.
32 devices in a mesh: rep: 4 (over x, core), shard: 8 (over z, y).
Axes of the slice: x: 2, y: 2, z: 4, core: 2. Of those that a mesh axis runs over, the one named last changes fastest.
Arguments:
- images: bfloat16 [32, 256, 1152], P(('rep', 'shard')), may hold values from -6 to 6
- cotangent: bfloat16 [32, 256, 1152], P(('rep', 'shard')), may hold values from -6 to 6
- w_qkv: bfloat16 [1152, 3456], P('shard'), may hold values from -2 to 2
- w_out: bfloat16 [1152, 1152], P('shard'), may hold values from -0.75 to 0.75
- w_up: bfloat16 [1152, 4304], P('shard'), may hold values from -0.1875 to 0.1875
- w_down: bfloat16 [1152, 4304], P('shard'), may hold values from -0.125 to 0.125
- vectors: bfloat16 [1152, 8], P('shard'), may hold values from -3 to 3, as said below
- up_bias: bfloat16 [4304], replicated, may hold values from -3 to 3
Outputs:
- outputs: bfloat16 [32, 256, 1152], P(('rep', 'shard'))
- input_grad: bfloat16 [32, 256, 1152], P(('rep', 'shard'))
- qkv_grad: float32 [1152, 3456], P('shard')
- out_grad: float32 [1152, 1152], P('shard')
- up_grad: float32 [1152, 4304], P('shard')
- down_grad: float32 [1152, 4304], P('shard')
- vectors_grad: float32 [1152, 8], P('shard')
- up_bias_grad: float32 [4304], replicated
Inputs may be any that keep to these rules, and one draw needn't show every extreme that they name: `vectors`: columns 0 and 5 (the norms' gains) are positive; the other columns have either sign.
All inputs are finite; a program needn't handle non-finite values.
Results may differ from a plain program's by a relative error of at most 0.014.
Values may be sent and summed in bfloat16 or wider, within the bound.
A program may use at most 256 MiB of HBM per device.

v0:
```python
import math
import jax
import jax.numpy as jnp
from jax import lax
from jax.sharding import PartitionSpec as P

HEAD_DIM = 72
EPSILON = 1e-06
GELU_COEF = 0.044715
ROOT_TWO_PI = math.sqrt(2.0 / math.pi)


def batched(pattern, left_op, right_op):
    return jnp.einsum(pattern, left_op, right_op, preferred_element_type=jnp.float32)


def contract_rows(left_op, right_op):
    return lax.dot_general(
        left_op, right_op, (((0,), (0,)), ((), ())), preferred_element_type=jnp.float32
    )


def contract_cols(left_op, right_op):
    return lax.dot_general(
        left_op, right_op, (((1,), (1,)), ((), ())), preferred_element_type=jnp.float32
    )


def norm_rows(hidden):
    row_mean = jnp.mean(hidden, axis=-1, keepdims=True)
    centered = hidden - row_mean
    variance = jnp.mean(centered * centered, axis=-1, keepdims=True)
    inv_std = lax.rsqrt(variance + EPSILON)
    return (centered * inv_std, inv_std)


def norm_back(grad_normed, normed, inv_std):
    mean_grad = jnp.mean(grad_normed, axis=-1, keepdims=True)
    mean_proj = jnp.mean(grad_normed * normed, axis=-1, keepdims=True)
    return inv_std * (grad_normed - mean_grad - normed * mean_proj)


def gelu_parts(pre_act):
    tanh_term = jnp.tanh(ROOT_TWO_PI * (pre_act + GELU_COEF * pre_act * pre_act * pre_act))
    activated = 0.5 * pre_act * (1.0 + tanh_term)
    derivative = 0.5 * (1.0 + tanh_term) + 0.5 * pre_act * (
        1.0 - tanh_term * tanh_term
    ) * ROOT_TWO_PI * (1.0 + 3.0 * GELU_COEF * pre_act * pre_act)
    return (activated, derivative)


def split_heads(tensor, batch_count, seq_len, head_size):
    return tensor.reshape(batch_count, seq_len, tensor.shape[-1] // head_size, head_size)


def forward_pass(images, w_qkv, w_out, w_up, w_down, vectors, up_bias):
    params = vectors.astype(jnp.float32)
    batch_count, seq_len, model_width = images.shape
    flat_rows = images.reshape(batch_count * seq_len, model_width).astype(jnp.float32)
    normed_one, inv_one = norm_rows(flat_rows)
    input_one = (normed_one * params[:, 0] + params[:, 1]).astype(jnp.bfloat16)
    projected = jnp.dot(input_one, w_qkv, preferred_element_type=jnp.float32)
    query = (projected[:, :model_width] + params[:, 2]).astype(jnp.bfloat16)
    keys_all = projected[:, model_width : 2 * model_width].astype(jnp.bfloat16)
    values_all = (projected[:, 2 * model_width :] + params[:, 3]).astype(jnp.bfloat16)
    score_scale = 1.0 / math.sqrt(HEAD_DIM)
    query_heads = split_heads(query, batch_count, seq_len, HEAD_DIM)
    key_heads = split_heads(keys_all, batch_count, seq_len, HEAD_DIM)
    value_heads = split_heads(values_all, batch_count, seq_len, HEAD_DIM)
    scores = batched("bqhd,bkhd->bhqk", query_heads, key_heads) * score_scale
    row_max = jnp.max(scores, axis=-1, keepdims=True)
    exponent = jnp.exp(scores - row_max)
    row_total = jnp.sum(exponent, axis=-1, keepdims=True)
    weights = (exponent / row_total).astype(jnp.bfloat16)
    logsum = row_max + jnp.log(row_total)
    attended = (
        batched("bhqk,bkhd->bqhd", weights, value_heads)
        .reshape(batch_count * seq_len, model_width)
        .astype(jnp.bfloat16)
    )
    middle = flat_rows + jnp.dot(attended, w_out, preferred_element_type=jnp.float32) + params[:, 4]
    normed_two, inv_two = norm_rows(middle)
    input_two = (normed_two * params[:, 5] + params[:, 6]).astype(jnp.bfloat16)
    pre_act = jnp.dot(input_two, w_up, preferred_element_type=jnp.float32) + up_bias.astype(
        jnp.float32
    )
    activated, derivative = gelu_parts(pre_act)
    act_bf = activated.astype(jnp.bfloat16)
    final = middle + contract_cols(act_bf, w_down) + params[:, 7]
    outputs = final.astype(jnp.bfloat16).reshape(batch_count, seq_len, model_width)
    saved = (
        normed_one,
        inv_one,
        input_one,
        query,
        keys_all,
        values_all,
        logsum,
        attended,
        normed_two,
        inv_two,
        input_two,
        derivative,
        act_bf,
    )
    return (outputs, saved)


def backward_pass(cotangent, saved, w_qkv, w_out, w_up, w_down, vectors):
    (
        normed_one,
        inv_one,
        input_one,
        query,
        keys_all,
        values_all,
        logsum,
        attended,
        normed_two,
        inv_two,
        input_two,
        derivative,
        act_bf,
    ) = saved
    params = vectors.astype(jnp.float32)
    batch_count, seq_len, model_width = cotangent.shape
    grad_bf = cotangent.reshape(batch_count * seq_len, model_width)
    grad_final = grad_bf.astype(jnp.float32)
    down_term = contract_rows(grad_bf, act_bf)
    grad_act = jnp.dot(grad_bf, w_down, preferred_element_type=jnp.float32)
    grad_pre = grad_act * derivative
    upb_term = jnp.sum(grad_pre, axis=0)
    grad_pre_bf = grad_pre.astype(jnp.bfloat16)
    up_term = contract_rows(input_two, grad_pre_bf)
    grad_two = contract_cols(grad_pre_bf, w_up)
    grad_gain_two = jnp.sum(grad_two * normed_two, axis=0)
    grad_bias_two = jnp.sum(grad_two, axis=0)
    grad_middle = grad_final + norm_back(grad_two * params[:, 5], normed_two, inv_two)
    grad_out_bias = jnp.sum(grad_middle, axis=0)
    grad_middle_bf = grad_middle.astype(jnp.bfloat16)
    out_term = contract_rows(attended, grad_middle_bf)
    grad_att = contract_cols(grad_middle_bf, w_out).astype(jnp.bfloat16)
    score_scale = 1.0 / math.sqrt(HEAD_DIM)
    query_heads = split_heads(query, batch_count, seq_len, HEAD_DIM)
    key_heads = split_heads(keys_all, batch_count, seq_len, HEAD_DIM)
    value_heads = split_heads(values_all, batch_count, seq_len, HEAD_DIM)
    grad_heads = split_heads(grad_att, batch_count, seq_len, HEAD_DIM)
    scores = batched("bqhd,bkhd->bhqk", query_heads, key_heads) * score_scale
    probs = jnp.exp(scores - logsum)
    probs_bf = probs.astype(jnp.bfloat16)
    grad_value = batched("bhqk,bqhd->bkhd", probs_bf, grad_heads)
    grad_prob = batched("bqhd,bkhd->bhqk", grad_heads, value_heads)
    delta = jnp.sum(probs * grad_prob, axis=-1, keepdims=True)
    grad_score = (probs * (grad_prob - delta) * score_scale).astype(jnp.bfloat16)
    grad_query = batched("bhqk,bkhd->bqhd", grad_score, key_heads)
    grad_key = batched("bhqk,bqhd->bkhd", grad_score, query_heads)
    flat_count = batch_count * seq_len
    grad_query = grad_query.reshape(flat_count, model_width)
    grad_key = grad_key.reshape(flat_count, model_width)
    grad_value = grad_value.reshape(flat_count, model_width)
    grad_qbias = jnp.sum(grad_query, axis=0)
    grad_vbias = jnp.sum(grad_value, axis=0)
    grad_proj = jnp.concatenate([grad_query, grad_key, grad_value], axis=1).astype(jnp.bfloat16)
    qkv_term = contract_rows(input_one, grad_proj)
    grad_one = contract_cols(grad_proj, w_qkv)
    grad_gain_one = jnp.sum(grad_one * normed_one, axis=0)
    grad_bias_one = jnp.sum(grad_one, axis=0)
    grad_input = grad_middle + norm_back(grad_one * params[:, 0], normed_one, inv_one)
    grad_down_bias = jnp.sum(grad_final, axis=0)
    vector_term = jnp.stack(
        [
            grad_gain_one,
            grad_bias_one,
            grad_qbias,
            grad_vbias,
            grad_out_bias,
            grad_gain_two,
            grad_bias_two,
            grad_down_bias,
        ],
        axis=1,
    )
    input_grad = grad_input.astype(jnp.bfloat16).reshape(batch_count, seq_len, model_width)
    return (input_grad, (qkv_term, out_term, up_term, down_term, vector_term), upb_term)


def per_device(images, cotangent, w_qkv, w_out, w_up, w_down, vectors, up_bias):
    whole = (
        lax.all_gather(w_qkv, "shard", axis=0, tiled=True),
        lax.all_gather(w_out, "shard", axis=0, tiled=True),
        lax.all_gather(w_up, "shard", axis=0, tiled=True),
        lax.all_gather(w_down, "shard", axis=0, tiled=True),
        lax.all_gather(vectors, "shard", axis=0, tiled=True),
    )
    outputs, saved = forward_pass(images, whole[0], whole[1], whole[2], whole[3], whole[4], up_bias)
    again = (
        lax.all_gather(w_qkv, "shard", axis=0, tiled=True),
        lax.all_gather(w_out, "shard", axis=0, tiled=True),
        lax.all_gather(w_up, "shard", axis=0, tiled=True),
        lax.all_gather(w_down, "shard", axis=0, tiled=True),
        lax.all_gather(vectors, "shard", axis=0, tiled=True),
    )
    input_grad, terms, upb_term = backward_pass(
        cotangent, saved, again[0], again[1], again[2], again[3], again[4]
    )
    upb_total = lax.psum(upb_term, ("rep", "shard"))
    owned = (
        lax.psum_scatter(terms[0], "shard", scatter_dimension=0, tiled=True),
        lax.psum_scatter(terms[1], "shard", scatter_dimension=0, tiled=True),
        lax.psum_scatter(terms[2], "shard", scatter_dimension=0, tiled=True),
        lax.psum_scatter(terms[3], "shard", scatter_dimension=0, tiled=True),
        lax.psum_scatter(terms[4], "shard", scatter_dimension=0, tiled=True),
    )
    parted = (
        lax.psum_scatter(owned[0], "rep", scatter_dimension=0, tiled=True),
        lax.psum_scatter(owned[1], "rep", scatter_dimension=0, tiled=True),
        lax.psum_scatter(owned[2], "rep", scatter_dimension=0, tiled=True),
        lax.psum_scatter(owned[3], "rep", scatter_dimension=0, tiled=True),
        lax.psum_scatter(owned[4], "rep", scatter_dimension=0, tiled=True),
    )
    summed = (
        lax.all_gather(parted[0], "rep", axis=0, tiled=True),
        lax.all_gather(parted[1], "rep", axis=0, tiled=True),
        lax.all_gather(parted[2], "rep", axis=0, tiled=True),
        lax.all_gather(parted[3], "rep", axis=0, tiled=True),
        lax.all_gather(parted[4], "rep", axis=0, tiled=True),
    )
    return (outputs, input_grad, summed[0], summed[1], summed[2], summed[3], summed[4], upb_total)


def solution(mesh):
    placed = (
        P(("rep", "shard"), None, None),
        P(("rep", "shard"), None, None),
        P("shard", None),
        P("shard", None),
        P("shard", None),
        P("shard", None),
        P("shard", None),
        P(),
    )
    return jax.shard_map(
        per_device,
        mesh=mesh,
        in_specs=placed,
        out_specs=(
            P(("rep", "shard"), None, None),
            P(("rep", "shard"), None, None),
            P("shard", None),
            P("shard", None),
            P("shard", None),
            P("shard", None),
            P("shard", None),
            P(),
        ),
        check_vma=False,
    )
```

profile of v0, /device:TPU:0, one launch (start us, length us, event | category | flops | bytes accessed | tf_op | source)
XLA Modules:
  0.0 1816.3 jit_solution(12791949931599254159)
XLA Ops:
  10.0 33.4 %all-gather = bf16[8,144,8]{1,2,0:T(8,128)(2,1)S(1)} all-gather(bf16[1,144,8]{1,2,0:T(8,128)(2,1)S(1)} %bitcast.145), channel_id=1, replica_groups=mesh['rep'=4,'shard'=8] {'shard'}, dimensions={0}, use_global_device_ids=true | all-gather | bytes 20736 | tf_op jit(solution)/shard_map/all_gather | solution.py:193
  45.3 86.9 %all-gather.14.cloned.1.call-done = bf16[1152,3456]{1,0:T(8,128)(2,1)} async-done(((bf16[144,3456]{1,0:T(8,128)(2,1)}), bf16[1152,3456]{1,0:T(8,128)(2,1)}) %all-gather.14.cloned.1.call-update) | async-done | bytes 7962640 | tf_op jit(solution)/shard_map/all_gather | solution.py:189
  132.2 6.0 fusion.88
  143.0 44.5 %all-gather.16.cloned.1.call-done = bf16[1152,1152]{1,0:T(8,128)(2,1)} async-done(((bf16[144,1152]{1,0:T(8,128)(2,1)}), bf16[1152,1152]{1,0:T(8,128)(2,1)}) %all-gather.16.cloned.1.call-update) | async-done | bytes 2654224 | tf_op jit(solution)/shard_map/all_gather | solution.py:190
  187.6 2.9 fusion.95
  190.8 142.4 %all-gather.18.cloned.1.call-done = bf16[1152,4304]{1,0:T(8,128)(2,1)} async-done(((bf16[144,4304]{1,0:T(8,128)(2,1)}), bf16[1152,4304]{1,0:T(8,128)(2,1)}) %all-gather.18.cloned.1.call-update) | async-done | bytes 9916432 | tf_op jit(solution)/shard_map/all_gather | solution.py:191
  333.2 8.3 convolution_add_fusion
  341.5 2.0 copy-done.2
  343.5 8.7 convolution_bitcast_fusion
  352.2 21.6 %copy.63 = f32[1152,4304]{1,0:T(8,128)} copy(f32[1152,4304]{0,1:T(8,128)} %convolution_bitcast_fusion) | data formatting | bytes 39665664
  373.9 104.3 %all-gather.20.cloned.1.call-done = bf16[1152,4304]{1,0:T(8,128)(2,1)} async-done(((bf16[144,4304]{1,0:T(8,128)(2,1)}), bf16[1152,4304]{1,0:T(8,128)(2,1)}) %all-gather.20.cloned.1.call-update) | async-done | bytes 9916432 | tf_op jit(solution)/shard_map/all_gather | solution.py:192
  478.2 10.5 fusion.98
  488.8 8.7 multiply_reduce_fusion.2
  499.4 3.2 fusion.74
  503.9 3.6 convolution_convert_fusion
  508.9 3.8 fusion.99
  512.7 9.1 fusion.51
  521.7 10.1 fusion.93
  531.8 4.2 fusion.92
  536.8 8.1 fusion.69
  545.7 11.5 fusion.65
  559.1 252.7 %reduce-scatter.24.cloned.1.call-done = f32[144,4304]{1,0:T(8,128)} async-done(((f32[1152,4304]{1,0:T(8,128)}), f32[144,4304]{1,0:T(8,128)}) %reduce-scatter.24.cloned.1.call-update) | async-done | bytes 2479120
  811.8 4.8 copy.64
  816.7 102.1 %reduce-scatter.20.cloned.1.call-done = f32[144,1152]{1,0:T(8,128)} async-done(((f32[1152,1152]{1,0:T(8,128)}), f32[144,1152]{1,0:T(8,128)}) %reduce-scatter.20.cloned.1.call-update) | async-done | bytes 663568 | tf_op jit(solution)/shard_map/reduce_scatter | solution.py:209
  918.8 271.9 %reduce-scatter.18.cloned.1.call-done = f32[144,3456]{1,0:T(8,128)} async-done(((f32[1152,3456]{1,0:T(8,128)}), f32[144,3456]{1,0:T(8,128)}) %reduce-scatter.18.cloned.1.call-update) | async-done | bytes 1990672 | tf_op jit(solution)/shard_map/reduce_scatter | solution.py:208
  1190.7 334.6 %reduce-scatter.22.cloned.1.call-done = f32[144,4304]{1,0:T(8,128)} async-done(((f32[1152,4304]{1,0:T(8,128)}), f32[144,4304]{1,0:T(8,128)}) %reduce-scatter.22.cloned.1.call-update) | async-done | bytes 2479120 | tf_op jit(solution)/shard_map/reduce_scatter | solution.py:210
  1525.3 103.3 %fusion.90 = (f32[48,3456]{1,0:T(8,128)}, f32[48,1152]{1,0:T(8,128)}, f32[40,4304]{1,0:T(8,128)}) fusion(f32[144,3456]{1,0:T(8,128)} %reduce-scatter.18.cloned.1.call-done, f32[144,1152]{1,0:T(8,128)} %reduce-scatter.20.cloned.1.call-done, f32[144,4304]{1,0:T(8,128)} %reduce-scatter.22.cloned.1.call-done), kind=kCustom, calls=%all-reduce-scatter.3 | all-reduce-scatter fusion | flops 1573378 | bytes 6707200
  1628.6 1.9 slice.58
  1630.5 2.6 collective-permute-start
  1633.2 8.0 fusion.61
  1646.8 7.0 concatenate.5
  1653.8 2.0 dynamic-slice_bitcast_fusion.2
  1656.9 8.6 collective-permute-start.2
  1666.7 5.1 concatenate.7
  1671.7 2.1 dynamic-slice_bitcast_fusion.1
  1674.9 4.3 dynamic-slice_bitcast_fusion
  1679.1 3.2 copy.57
  1682.4 9.5 fusion.23
  1692.0 6.7 collective-permute-start.1
  1699.9 39.3 %psum.7 = f32[4304]{0:T(1024)} all-reduce(f32[4304]{0:T(1024)S(1)} %copy-done.34), channel_id=1, replica_groups=mesh['rep'=4,'shard'=8] {'rep','shard'}, use_global_device_ids=true, to_apply=%region_30.0 | all-reduce | flops 4304 | bytes 34432 | tf_op jit(solution)/shard_map/psum | solution.py:206
  1740.1 7.1 all-reduce.4
  1747.3 5.2 all-gather.5
  1753.5 10.2 all-gather.2
  1764.6 2.6 reshape.196
  1767.2 10.4 all-gather.24.cloned.1.call-done
  1777.7 2.9 reshape.200
  1780.6 25.7 %all-gather.26.cloned.1.call-done = f32[4,36,4304]{2,1,0:T(8,128)} async-done(((f32[1,36,4304]{2,1,0:T(8,128)}), f32[4,36,4304]{2,1,0:T(8,128)}) %all-gather.26.cloned.1.call-update) | async-done | bytes 2479120 | tf_op jit(solution)/shard_map/all_gather | solution.py:225
  1806.3 2.9 reshape.202
  (163 shorter events, 28.9 us)
Async XLA Ops:
  7.2 2.9 copy-start.39
  7.2 36.4 %copy-start.36 = (bf16[4304]{0:T(1024)(128)(2,1)S(1)}, bf16[4304]{0:T(1024)(128)(2,1)}, u32[]{:S(2)}) copy-start(bf16[4304]{0:T(1024)(128)(2,1)} %param.15) | copy-start | bytes 25828
  7.2 37.6 %copy-start.1 = (bf16[1,256,1152]{2,1,0:T(8,128)(2,1)S(1)}, bf16[1,256,1152]{2,1,0:T(8,128)(2,1)}, u32[]{:S(2)}) copy-start(bf16[1,256,1152]{2,1,0:T(8,128)(2,1)} %param.8) | copy-start | bytes 1769476
  7.2 125.0 %all-gather.14.cloned.1.call-start = ((), (), s32[]{:S(2)}) async-start(), calls=%async_computation.5 | async-start | bytes 8957952 | tf_op jit(solution)/shard_map/all_gather | solution.py:189
  7.9 179.6 %all-gather.16.cloned.1.call-start = ((), (), s32[]{:S(2)}) async-start(), calls=%async_computation.6 | async-start | bytes 2985984 | tf_op jit(solution)/shard_map/all_gather | solution.py:190
  8.7 324.5 %all-gather.18.cloned.1.call-start = ((), (), s32[]{:S(2)}) async-start(), calls=%async_computation.7 | async-start | bytes 11280384 | tf_op jit(solution)/shard_map/all_gather | solution.py:191
  9.4 468.8 %all-gather.20.cloned.1.call-start = ((), (), s32[]{:S(2)}) async-start(), calls=%async_computation.8 | async-start | bytes 11280384 | tf_op jit(solution)/shard_map/all_gather | solution.py:192
  10.0 801.8 %reduce-scatter.24.cloned.1.call-start = ((), (), s32[]{:S(2)}) async-start(), calls=%async_computation.15 | async-start | bytes 22560768
  44.8 93.4 %copy-start.20 = (f32[1152]{0:T(1024)}, f32[1152]{0:T(1024)S(1)}, u32[]{:S(2)}) copy-start(f32[1152]{0:T(1024)S(1)} %get-tuple-element.22) | copy-start | bytes 13828
  45.0 93.2 %copy-start.26 = (f32[256]{0:T(256)}, f32[256]{0:T(256)S(1)}, u32[]{:S(2)}) copy-start(f32[256]{0:T(256)S(1)} %broadcast_multiply_fusion.5) | copy-start | bytes 3076
  45.3 92.9 %copy-start.31 = (f32[256]{0:T(256)}, f32[256]{0:T(256)S(1)}, u32[]{:S(2)}) copy-start(f32[256]{0:T(256)S(1)} %add_rsqrt_fusion.1) | copy-start | bytes 3076
  138.7 2.1 copy-start.7
  140.0 3.0 copy-start.16
  140.8 2.2 copy-start.22
  142.0 45.6 %copy-start.38 = (f32[1152]{0:T(1024)S(1)}, f32[1152]{0:T(1024)}, u32[]{:S(2)}) copy-start(f32[1152]{0:T(1024)} %get-tuple-element.19) | copy-start | bytes 13828
  143.0 47.4 %copy-start.11 = (bf16[16,72,256]{2,1,0:T(8,128)(2,1)}, bf16[16,72,256]{2,1,0:T(8,128)(2,1)S(1)}, u32[]{:S(2)}) copy-start(bf16[16,72,256]{2,1,0:T(8,128)(2,1)S(1)} %fusion.50) | copy-start | bytes 1769476
  187.6 145.6 %copy-start.18 = (f32[1152]{0:T(1024)S(1)}, f32[1152]{0:T(1024)}, u32[]{:S(2)}) copy-start(f32[1152]{0:T(1024)} %get-tuple-element.18) | copy-start | bytes 13828
  187.6 145.6 %copy-start.35 = (f32[4304]{0:T(1024)S(1)}, f32[4304]{0:T(1024)}, u32[]{:S(2)}) copy-start(f32[4304]{0:T(1024)} %convert_element_type.84) | copy-start | bytes 51652
  190.5 298.3 %copy-start.24 = (f32[256]{0:T(256)}, f32[256]{0:T(256)S(1)}, u32[]{:S(2)}) copy-start(f32[256]{0:T(256)S(1)} %broadcast_multiply_fusion.4) | copy-start | bytes 3076
  190.8 298.0 %copy-start.29 = (f32[256]{0:T(256)}, f32[256]{0:T(256)S(1)}, u32[]{:S(2)}) copy-start(f32[256]{0:T(256)S(1)} %add_rsqrt_fusion) | copy-start | bytes 3076
  333.2 10.4 copy-start.3
  341.5 2.1 copy-start.2
  373.9 544.9 %reduce-scatter.20.cloned.1.call-start = ((), (), s32[]{:S(2)}) async-start(), calls=%async_computation.10 | async-start | bytes 5971968 | tf_op jit(solution)/shard_map/reduce_scatter | solution.py:209
  488.8 8.7 copy-start.9
  502.6 688.1 %reduce-scatter.18.cloned.1.call-start = ((), (), s32[]{:S(2)}) async-start(), calls=%async_computation.9 | async-start | bytes 17915904 | tf_op jit(solution)/shard_map/reduce_scatter | solution.py:208
  531.8 5.0 copy-start.14
  531.8 5.0 copy-start.15
  531.8 5.0 copy-start.21
  531.8 5.0 copy-start.27
  531.8 5.0 copy-start.32
  545.0 980.4 %reduce-scatter.22.cloned.1.call-start = ((), (), s32[]{:S(2)}) async-start(), calls=%async_computation.11 | async-start | bytes 22560768 | tf_op jit(solution)/shard_map/reduce_scatter | solution.py:210
  557.2 1117.7 %all-reduce.11.cloned.1.call-start = ((), (), s32[]{:S(2)}) async-start(), calls=%async_computation.17 | async-start | bytes 8814592
  816.6 816.5 %copy-start.5 = (bf16[1,256,16,72]{1,3,2,0:T(8,128)(2,1)S(1)}, bf16[1,256,16,72]{1,3,2,0:T(8,128)(2,1)}, u32[]{:S(2)}) copy-start(bf16[1,256,16,72]{1,3,2,0:T(8,128)(2,1)} %copy-done.4) | copy-start | bytes 1769476
  816.6 816.5 %copy-start.28 = (f32[256]{0:T(256)S(1)}, f32[256]{0:T(256)}, u32[]{:S(2)}) copy-start(f32[256]{0:T(256)} %copy-done.26) | copy-start | bytes 3076
  816.7 816.5 %copy-start.33 = (f32[256]{0:T(256)S(1)}, f32[256]{0:T(256)}, u32[]{:S(2)}) copy-start(f32[256]{0:T(256)} %copy-done.31) | copy-start | bytes 3076
  816.7 922.5 %reduce-scatter.26.cloned.1.call-start = ((), (), s32[]{:S(2)}) async-start(), calls=%async_computation.16 | async-start | bytes 663552
  1630.5 16.3 collective-permute-start
  1646.8 117.8 %all-gather.22.cloned.1.call-start = ((), (), s32[]{:S(2)}) async-start(), calls=%async_computation.12 | async-start | bytes 2764800 | tf_op jit(solution)/shard_map/all_gather | solution.py:222
  1655.9 121.8 %all-gather.24.cloned.1.call-start = ((), (), s32[]{:S(2)}) async-start(), calls=%async_computation.13 | async-start | bytes 3481600 | tf_op jit(solution)/shard_map/all_gather | solution.py:224
  1656.9 9.8 collective-permute-start.2
  1673.8 132.5 %all-gather.26.cloned.1.call-start = ((), (), s32[]{:S(2)}) async-start(), calls=%async_computation.14 | async-start | bytes 3481600 | tf_op jit(solution)/shard_map/all_gather | solution.py:225
  1679.1 3.2 copy-start.42
  1679.1 3.2 copy-start.41
  1679.1 3.3 copy-start.37
  1682.4 9.5 copy-start.10
  1682.4 16.2 copy-start.13
  1691.9 8.0 copy-start.34
  1692.0 61.2 %collective-permute-start.1 = (f32[36,1152]{1,0:T(8,128)S(1)}, f32[36,1152]{1,0:T(8,128)S(1)}, u32[]{:S(2)}, u32[]{:S(2)}) collective-permute-start(f32[36,1152]{1,0:T(8,128)S(1)} %slice.59), channel_id=1, source_target_pairs={{0,8},{8,16},{16,24},{1,9},{9,17},{17,25},{2,10},{10,18},{18,26},{... | collective-permute-start | bytes 497672
  (11 other events, 11.5 us)
Sparse Core Ops, SparseCore 0:
  10.2 121.9 all-gather.13
  134.4 53.1 all-gather.15
  189.7 143.3 all-gather.17
  335.2 142.9 all-gather.19
  482.0 329.7 reduce-scatter.23
  815.2 103.5 reduce-scatter.19
  922.7 268.0 reduce-scatter.17
  1194.7 330.6 reduce-scatter.21
  1527.8 129.9 all-reduce.10
  1660.9 63.1 reduce-scatter.25
  1725.6 22.8 all-gather.21
  1749.9 27.6 all-gather.23
  1779.2 27.0 all-gather.25
where the time goes:
time: 1820 us
  waiting for transfers between devices  1380 us (76%)
  blocking collectives  198 us (11%)
  matrix products  118 us (6%)
  local copies, waits for them, and re-layouts  79 us (4%)
  starting transfers between devices  19.1 us (1%)
    reduce_scatter x1, waiting for transfers between devices, per_device(): lax.psum_scatter(terms[2], 'shard', scatter_dimension=0, tiled=True)  335 us
    reduce_scatter x1, waiting for transfers between devices, per_device(): lax.psum_scatter(terms[0], 'shard', scatter_dimension=0, tiled=True)  272 us
    unnamed x19, waiting for transfers between devices  256 us
    all_gather x1, waiting for transfers between devices, per_device(): lax.all_gather(w_up, 'shard', axis=0, tiled=True)  142 us
    unnamed x2, blocking collectives  110 us
    all_gather x1, waiting for transfers between devices, per_device(): lax.all_gather(w_down, 'shard', axis=0, tiled=True)  104 us
    reduce_scatter x1, waiting for transfers between devices, per_device(): lax.psum_scatter(terms[1], 'shard', scatter_dimension=0, tiled=True)  102 us
    all_gather x1, waiting for transfers between devices, per_device(): lax.all_gather(w_qkv, 'shard', axis=0, tiled=True)  86.9 us
  transfers between devices with their start and end apart: 16, of which 11 were waited for; matrix products, arithmetic and copies ran while one was open for 16% of the time, Pallas kernels for 0%

commit v1 on v0

--- a/solution.py
+++ b/solution.py
@@ -8,6 +8,27 @@
 EPSILON = 1e-06
 GELU_COEF = 0.044715
 ROOT_TWO_PI = math.sqrt(2.0 / math.pi)
+
+
+def ring_gather(array, axis, dim):
+    size, mine, span = (lax.axis_size(axis), lax.axis_index(axis), array.shape[dim])
+    forward = [(i, (i + 1) % size) for i in range(size)]
+    left = [(i, (i - 1) % size) for i in range(size)]
+    whole = jnp.zeros((*array.shape[:dim], size * span, *array.shape[dim + 1 :]), array.dtype)
+    whole = lax.dynamic_update_slice_in_dim(whole, array, mine * span, axis=dim)
+    from_left = from_right = array
+    middle = size // 2
+    for hop in range(1, middle + 1):
+        from_left = lax.ppermute(from_left, axis, forward)
+        whole = lax.dynamic_update_slice_in_dim(
+            whole, from_left, (mine - hop) % size * span, axis=dim
+        )
+        if hop < size - middle:
+            from_right = lax.ppermute(from_right, axis, left)
+            whole = lax.dynamic_update_slice_in_dim(
+                whole, from_right, (mine + hop) % size * span, axis=dim
+            )
+    return whole
 
 
 def batched(pattern, left_op, right_op):
@@ -188,7 +209,7 @@
     whole = (
         lax.all_gather(w_qkv, "shard", axis=0, tiled=True),
         lax.all_gather(w_out, "shard", axis=0, tiled=True),
-        lax.all_gather(w_up, "shard", axis=0, tiled=True),
+        ring_gather(w_up, "shard", 0),
         lax.all_gather(w_down, "shard", axis=0, tiled=True),
         lax.all_gather(vectors, "shard", axis=0, tiled=True),
     )

time: 1820 us -> 1940 us (1.066)
  waiting for transfers between devices: 1380 us -> 1440 us
  starting transfers between devices: 19.1 us -> 42.9 us
    ppermute x0 -> x7, waiting for transfers between devices: none -> 140 us  [the longest x4 112 us: ring_gather(): from_left = lax.ppermute(from_left, axis, forward)]
    all_gather x1, waiting for transfers between devices: 86.9 us -> 0.01 us  [per_device(): lax.all_gather(w_qkv, 'shard', axis=0, tiled=True)]
    unnamed x19, waiting for transfers between devices: 256 us -> 331 us
    all_gather x1, blocking collectives: 33.4 us -> 87.2 us  [per_device(): lax.all_gather(vectors, 'shard', axis=0, tiled=True)]
    unnamed x2, blocking collectives: 110 us -> 64.2 us
    all_gather x1, waiting for transfers between devices: 44.5 us -> 17.3 us  [per_device(): lax.all_gather(w_out, 'shard', axis=0, tiled=True)]
    all_gather x1, waiting for transfers between devices: 25.7 us -> 0.01 us  [per_device(): lax.all_gather(parted[3], 'rep', axis=0, tiled=True)]
    ppermute x0 -> x7, starting transfers between devices: none -> 19.6 us  [the longest x3 11 us: ring_gather(): from_right = lax.ppermute(from_right, axis, left)]
  transfers between devices with their start and end apart: 16 -> 23, of which waited for: 11 -> 14; matrix products, arithmetic and copies ran while one was open for 16% -> 14% of each run, Pallas kernels for 0% -> 0%
where the time goes in v1:
time: 1940 us; the launch traced here: 1930 us
  waiting for transfers between devices  1440 us (74%)
  blocking collectives  207 us (11%)
  matrix products  119 us (6%)
  local copies, waits for them, and re-layouts  97.4 us (5%)
  starting transfers between devices  42.9 us (2%)
    reduce_scatter x1, waiting for transfers between devices, per_device(): lax.psum_scatter(terms[2], 'shard', scatter_dimension=0, tiled=True)  335 us
    unnamed x19, waiting for transfers between devices  331 us
    reduce_scatter x1, waiting for transfers between devices, per_device(): lax.psum_scatter(terms[0], 'shard', scatter_dimension=0, tiled=True)  272 us
    all_gather x1, waiting for transfers between devices, per_device(): lax.all_gather(w_up, 'shard', axis=0, tiled=True)  141 us
    ppermute x4, waiting for transfers between devices, ring_gather(): from_left = lax.ppermute(from_left, axis, forward)  112 us
    all_gather x1, waiting for transfers between devices, per_device(): lax.all_gather(w_down, 'shard', axis=0, tiled=True)  101 us
    reduce_scatter x1, waiting for transfers between devices, per_device(): lax.psum_scatter(terms[1], 'shard', scatter_dimension=0, tiled=True)  101 us
    all_gather x1, blocking collectives, per_device(): lax.all_gather(vectors, 'shard', axis=0, tiled=True)  87.2 us
  transfers between devices with their start and end apart: 23, of which 14 were waited for; matrix products, arithmetic and copies ran while one was open for 14% of the time, Pallas kernels for 0%

profile of v1, /device:TPU:0, one launch (start us, length us, event | category | flops | bytes accessed | tf_op | source)
XLA Modules:
  0.0 1928.2 jit_solution(17755222769274136291)
XLA Ops:
  9.4 3.0 collective-permute-start
  12.5 3.1 collective-permute-start.1
  16.8 87.2 %all-gather = bf16[8,144,8]{1,2,0:T(8,128)(2,1)S(1)} all-gather(bf16[1,144,8]{1,2,0:T(8,128)(2,1)} %bitcast.145), channel_id=1, replica_groups=mesh['rep'=4,'shard'=8] {'shard'}, dimensions={0}, use_global_device_ids=true | all-gather | bytes 20736 | tf_op jit(solution)/shard_map/all_gather | solution.py:214
  104.9 4.5 broadcast_in_dim.2
  110.5 4.5 collective-permute-start.3
  116.3 68.4 %collective-permute-done.2 = bf16[144,4304]{1,0:T(8,128)(2,1)} collective-permute-done((bf16[144,4304]{1,0:T(8,128)(2,1)}, bf16[144,4304]{1,0:T(8,128)(2,1)}, u32[]{:S(2)}, u32[]{:S(2)}) %collective-permute-start.2) | collective-permute-done | bytes 1239584 | tf_op jit(solution)/shard_map/ppermute | solution.py:22
  194.2 3.4 collective-permute-start.5
  200.1 31.7 %collective-permute-done.4 = bf16[144,4304]{1,0:T(8,128)(2,1)S(1)} collective-permute-done((bf16[144,4304]{1,0:T(8,128)(2,1)}, bf16[144,4304]{1,0:T(8,128)(2,1)S(1)}, u32[]{:S(2)}, u32[]{:S(2)}) %collective-permute-start.4) | collective-permute-done | bytes 1239584 | tf_op jit(solution)/shard_map/ppermute | solution.py:22
  236.8 26.1 %collective-permute-done.5 = bf16[144,4304]{1,0:T(8,128)(2,1)S(1)} collective-permute-done((bf16[144,4304]{1,0:T(8,128)(2,1)S(1)}, bf16[144,4304]{1,0:T(8,128)(2,1)S(1)}, u32[]{:S(2)}, u32[]{:S(2)}) %collective-permute-start.5) | collective-permute-done | bytes 1239584 | tf_op jit(solution)/shard_map/ppermute | solution.py:27
  264.0 11.8 collective-permute-done.6
  277.0 6.3 fusion.88
  288.3 17.3 all-gather.16.cloned.1.call-done
  308.8 8.0 convolution_add_fusion
  318.8 8.7 convolution_bitcast_fusion
  327.6 21.6 %copy.63 = f32[1152,4304]{1,0:T(8,128)} copy(f32[1152,4304]{0,1:T(8,128)} %convolution_bitcast_fusion) | data formatting | bytes 39665664
  349.9 101.4 %all-gather.18.cloned.1.call-done = bf16[1152,4304]{1,0:T(8,128)(2,1)} async-done(((bf16[144,4304]{1,0:T(8,128)(2,1)}), bf16[1152,4304]{1,0:T(8,128)(2,1)}) %all-gather.18.cloned.1.call-update) | async-done | bytes 9916432 | tf_op jit(solution)/shard_map/all_gather | solution.py:213
  451.2 11.4 fusion.98
  462.6 322.3 %reduce-scatter.24.cloned.1.call-done = f32[144,4304]{1,0:T(8,128)} async-done(((f32[1152,4304]{1,0:T(8,128)}), f32[144,4304]{1,0:T(8,128)}) %reduce-scatter.24.cloned.1.call-update) | async-done | bytes 2479120
  784.9 4.8 copy.64
  789.8 141.0 %all-gather.20.cloned.1.call-done = bf16[1152,4304]{1,0:T(8,128)(2,1)} async-done(((bf16[144,4304]{1,0:T(8,128)(2,1)}), bf16[1152,4304]{1,0:T(8,128)(2,1)}) %all-gather.20.cloned.1.call-update) | async-done | bytes 9916432 | tf_op jit(solution)/shard_map/all_gather | solution.py:220
  930.8 8.6 multiply_reduce_fusion.2
  941.3 3.2 fusion.74
  945.9 3.7 convolution_convert_fusion
  950.8 3.7 fusion.99
  954.6 9.1 fusion.51
  963.6 9.6 fusion.93
  973.3 3.9 fusion.92
  978.0 9.0 fusion.69
  987.7 11.5 fusion.65
  1001.2 8.1 fusion.61
  1014.9 5.5 all-reduce.11.cloned.1.call-done
  1020.4 4.2 dynamic-slice_bitcast_fusion
  1024.6 3.1 copy.57
  1027.8 100.7 %reduce-scatter.20.cloned.1.call-done = f32[144,1152]{1,0:T(8,128)} async-done(((f32[1152,1152]{1,0:T(8,128)}), f32[144,1152]{1,0:T(8,128)}) %reduce-scatter.20.cloned.1.call-update) | async-done | bytes 663568 | tf_op jit(solution)/shard_map/reduce_scatter | solution.py:230
  1128.6 271.9 %reduce-scatter.18.cloned.1.call-done = f32[144,3456]{1,0:T(8,128)} async-done(((f32[1152,3456]{1,0:T(8,128)}), f32[144,3456]{1,0:T(8,128)}) %reduce-scatter.18.cloned.1.call-update) | async-done | bytes 1990672 | tf_op jit(solution)/shard_map/reduce_scatter | solution.py:229
  1400.5 334.6 %reduce-scatter.22.cloned.1.call-done = f32[144,4304]{1,0:T(8,128)} async-done(((f32[1152,4304]{1,0:T(8,128)}), f32[144,4304]{1,0:T(8,128)}) %reduce-scatter.22.cloned.1.call-update) | async-done | bytes 2479120 | tf_op jit(solution)/shard_map/reduce_scatter | solution.py:231
  1735.1 58.0 %fusion.90 = (f32[48,3456]{1,0:T(8,128)}, f32[48,1152]{1,0:T(8,128)S(1)}, f32[40,4304]{1,0:T(8,128)}) fusion(f32[144,3456]{1,0:T(8,128)} %reduce-scatter.18.cloned.1.call-done, f32[144,1152]{1,0:T(8,128)} %reduce-scatter.20.cloned.1.call-done, f32[144,4304]{1,0:T(8,128)} %reduce-scatter.22.cloned.1.call-done), kind=kCustom, calls=%all-reduce-scatter.3 | all-reduce-scatter fusion | flops 1573378 | bytes 6707200
  1798.2 7.0 concatenate.5
  1808.2 9.5 collective-permute-start.9
  1818.3 6.0 concatenate.7
  1826.5 9.4 fusion.23
  1836.0 10.6 collective-permute-start.8
  1847.9 42.1 %psum.7 = f32[4304]{0:T(1024)} all-reduce(f32[4304]{0:T(1024)S(1)} %copy-done.33), channel_id=1, replica_groups=mesh['rep'=4,'shard'=8] {'rep','shard'}, use_global_device_ids=true, to_apply=%region_30.31 | all-reduce | flops 4304 | bytes 34432 | tf_op jit(solution)/shard_map/psum | solution.py:227
  1890.9 6.1 all-reduce.4
  1897.1 5.3 all-gather.5
  1903.3 8.8 all-gather.2
  1913.0 2.9 reshape.202
  1918.5 2.9 reshape.200
  (178 shorter events, 66.2 us)
Async XLA Ops:
  7.2 97.4 %copy-start.1 = (bf16[1,256,1152]{2,1,0:T(8,128)(2,1)S(1)}, bf16[1,256,1152]{2,1,0:T(8,128)(2,1)}, u32[]{:S(2)}) copy-start(bf16[1,256,1152]{2,1,0:T(8,128)(2,1)} %param.8) | copy-start | bytes 1769476
  7.2 269.8 %all-gather.14.cloned.1.call-start = ((), (), s32[]{:S(2)}) async-start(), calls=%async_computation.5 | async-start | bytes 8957952 | tf_op jit(solution)/shard_map/all_gather | solution.py:210
  7.9 297.7 %all-gather.16.cloned.1.call-start = ((), (), s32[]{:S(2)}) async-start(), calls=%async_computation.6 | async-start | bytes 2985984 | tf_op jit(solution)/shard_map/all_gather | solution.py:211
  8.7 442.6 %all-gather.18.cloned.1.call-start = ((), (), s32[]{:S(2)}) async-start(), calls=%async_computation.7 | async-start | bytes 11280384 | tf_op jit(solution)/shard_map/all_gather | solution.py:213
  9.4 775.5 %reduce-scatter.24.cloned.1.call-start = ((), (), s32[]{:S(2)}) async-start(), calls=%async_computation.15 | async-start | bytes 22560768
  9.4 94.7 %collective-permute-start = (bf16[144,4304]{1,0:T(8,128)(2,1)}, bf16[144,4304]{1,0:T(8,128)(2,1)}, u32[]{:S(2)}, u32[]{:S(2)}) collective-permute-start(bf16[144,4304]{1,0:T(8,128)(2,1)} %param.12), channel_id=1, source_target_pairs={{0,1},{1,2},{2,3},{3,4},{4,5},{5,6},{6,7},{7,0},{8,9},{9,10},{10,1... | collective-permute-start | bytes 3718664 | tf_op jit(solution)/shard_map/ppermute | solution.py:22
  12.5 98.0 %collective-permute-start.1 = (bf16[144,4304]{1,0:T(8,128)(2,1)}, bf16[144,4304]{1,0:T(8,128)(2,1)}, u32[]{:S(2)}, u32[]{:S(2)}) collective-permute-start(bf16[144,4304]{1,0:T(8,128)(2,1)} %param.12), channel_id=1, source_target_pairs={{0,7},{1,0},{2,1},{3,2},{4,3},{5,4},{6,5},{7,6},{8,15},{9,8},{10,9... | collective-permute-start | bytes 3718664 | tf_op jit(solution)/shard_map/ppermute | solution.py:27
  104.2 80.5 %collective-permute-start.2 = (bf16[144,4304]{1,0:T(8,128)(2,1)}, bf16[144,4304]{1,0:T(8,128)(2,1)}, u32[]{:S(2)}, u32[]{:S(2)}) collective-permute-start(bf16[144,4304]{1,0:T(8,128)(2,1)} %collective-permute-done), channel_id=1, source_target_pairs={{0,1},{1,2},{2,3},{3,4},{4,5},{5,6},{6,7},{7,0},{8,9},{9,10},{10,1... | collective-permute-start | bytes 3718664 | tf_op jit(solution)/shard_map/ppermute | solution.py:22
  104.5 172.4 %copy-start.25 = (f32[256]{0:T(256)}, f32[256]{0:T(256)S(1)}, u32[]{:S(2)}) copy-start(f32[256]{0:T(256)S(1)} %broadcast_multiply_fusion.5) | copy-start | bytes 3076
  104.9 172.1 %copy-start.30 = (f32[256]{0:T(256)}, f32[256]{0:T(256)S(1)}, u32[]{:S(2)}) copy-start(f32[256]{0:T(256)S(1)} %add_rsqrt_fusion.1) | copy-start | bytes 3076
  104.9 4.5 copy-start.3
  104.9 10.8 copy-start.35
  110.5 83.7 %collective-permute-start.3 = (bf16[144,4304]{1,0:T(8,128)(2,1)}, bf16[144,4304]{1,0:T(8,128)(2,1)S(1)}, u32[]{:S(2)}, u32[]{:S(2)}) collective-permute-start(bf16[144,4304]{1,0:T(8,128)(2,1)} %collective-permute-done.1), channel_id=1, source_target_pairs={{0,7},{1,0},{2,1},{3,2},{4,3},{5,4},{6,5},{7,6},{8,15},{9,8},{10,9... | collective-permute-start | bytes 3718664 | tf_op jit(solution)/shard_map/ppermute | solution.py:27
  115.7 161.3 %copy-start.19 = (f32[1152]{0:T(1024)}, f32[1152]{0:T(1024)S(1)}, u32[]{:S(2)}) copy-start(f32[1152]{0:T(1024)S(1)} %get-tuple-element.22) | copy-start | bytes 13828
  184.7 47.1 %collective-permute-start.4 = (bf16[144,4304]{1,0:T(8,128)(2,1)}, bf16[144,4304]{1,0:T(8,128)(2,1)S(1)}, u32[]{:S(2)}, u32[]{:S(2)}) collective-permute-start(bf16[144,4304]{1,0:T(8,128)(2,1)} %collective-permute-done.2), channel_id=1, source_target_pairs={{0,1},{1,2},{2,3},{3,4},{4,5},{5,6},{6,7},{7,0},{8,9},{9,10},{10,1... | collective-permute-start | bytes 3718664 | tf_op jit(solution)/shard_map/ppermute | solution.py:22
  194.2 68.7 %collective-permute-start.5 = (bf16[144,4304]{1,0:T(8,128)(2,1)S(1)}, bf16[144,4304]{1,0:T(8,128)(2,1)S(1)}, u32[]{:S(2)}, u32[]{:S(2)}) collective-permute-start(bf16[144,4304]{1,0:T(8,128)(2,1)S(1)} %collective-permute-done.3), channel_id=1, source_target_pairs={{0,7},{1,0},{2,1},{3,2},{4,3},{5,4},{6,5},{7,6},{8,15},{9,8},{10,9... | collective-permute-start | bytes 3718664 | tf_op jit(solution)/shard_map/ppermute | solution.py:27
  231.8 44.0 %collective-permute-start.6 = (bf16[144,4304]{1,0:T(8,128)(2,1)S(1)}, bf16[144,4304]{1,0:T(8,128)(2,1)S(1)}, u32[]{:S(2)}, u32[]{:S(2)}) collective-permute-start(bf16[144,4304]{1,0:T(8,128)(2,1)S(1)} %collective-permute-done.4), channel_id=1, source_target_pairs={{0,1},{1,2},{2,3},{3,4},{4,5},{5,6},{6,7},{7,0},{8,9},{9,10},{10,1... | collective-permute-start | bytes 3718664 | tf_op jit(solution)/shard_map/ppermute | solution.py:22
  285.1 2.1 copy-start
  285.1 3.1 copy-start.15
  285.9 2.4 copy-start.21
  288.3 28.5 %copy-start.10 = (bf16[16,72,256]{2,1,0:T(8,128)(2,1)}, bf16[16,72,256]{2,1,0:T(8,128)(2,1)S(1)}, u32[]{:S(2)}) copy-start(bf16[16,72,256]{2,1,0:T(8,128)(2,1)S(1)} %fusion.50) | copy-start | bytes 1769476
  288.3 20.5 %copy-start.17 = (f32[1152]{0:T(1024)S(1)}, f32[1152]{0:T(1024)}, u32[]{:S(2)}) copy-start(f32[1152]{0:T(1024)} %get-tuple-element.18) | copy-start | bytes 13828
  288.3 20.5 %copy-start.34 = (f32[4304]{0:T(1024)S(1)}, f32[4304]{0:T(1024)}, u32[]{:S(2)}) copy-start(f32[4304]{0:T(1024)} %convert_element_type.84) | copy-start | bytes 51652
  308.5 622.3 %copy-start.23 = (f32[256]{0:T(256)}, f32[256]{0:T(256)S(1)}, u32[]{:S(2)}) copy-start(f32[256]{0:T(256)S(1)} %broadcast_multiply_fusion.4) | copy-start | bytes 3076
  308.8 622.0 %copy-start.28 = (f32[256]{0:T(256)}, f32[256]{0:T(256)S(1)}, u32[]{:S(2)}) copy-start(f32[256]{0:T(256)S(1)} %add_rsqrt_fusion) | copy-start | bytes 3076
  308.8 10.0 copy-start.4
  349.2 581.5 %all-gather.20.cloned.1.call-start = ((), (), s32[]{:S(2)}) async-start(), calls=%async_computation.8 | async-start | bytes 11280384 | tf_op jit(solution)/shard_map/all_gather | solution.py:220
  349.8 670.6 %all-reduce.11.cloned.1.call-start = ((), (), s32[]{:S(2)}) async-start(), calls=%async_computation.17 | async-start | bytes 8814592
  789.7 338.8 %reduce-scatter.20.cloned.1.call-start = ((), (), s32[]{:S(2)}) async-start(), calls=%async_computation.10 | async-start | bytes 5971968 | tf_op jit(solution)/shard_map/reduce_scatter | solution.py:230
  944.5 455.9 %reduce-scatter.18.cloned.1.call-start = ((), (), s32[]{:S(2)}) async-start(), calls=%async_computation.9 | async-start | bytes 17915904 | tf_op jit(solution)/shard_map/reduce_scatter | solution.py:229
  973.3 4.7 copy-start.13
  973.3 4.7 copy-start.14
  973.3 4.7 copy-start.20
  973.3 4.7 copy-start.26
  973.3 4.7 copy-start.31
  987.0 748.1 %reduce-scatter.22.cloned.1.call-start = ((), (), s32[]{:S(2)}) async-start(), calls=%async_computation.11 | async-start | bytes 22560768 | tf_op jit(solution)/shard_map/reduce_scatter | solution.py:231
  999.2 890.7 %reduce-scatter.26.cloned.1.call-start = ((), (), s32[]{:S(2)}) async-start(), calls=%async_computation.16 | async-start | bytes 663552
  1014.8 898.2 %all-gather.26.cloned.1.call-start = ((), (), s32[]{:S(2)}) async-start(), calls=%async_computation.14 | async-start | bytes 3481600 | tf_op jit(solution)/shard_map/all_gather | solution.py:246
  1027.8 888.1 %all-gather.22.cloned.1.call-start = ((), (), s32[]{:S(2)}) async-start(), calls=%async_computation.12 | async-start | bytes 2764800 | tf_op jit(solution)/shard_map/all_gather | solution.py:243
  1795.0 3.2 collective-permute-start.7
  1805.2 21.2 %copy-start.38 = (f32[256]{0:T(256)S(1)}, f32[256]{0:T(256)}, u32[]{:S(2)}) copy-start(f32[256]{0:T(256)} %get-tuple-element.11) | copy-start | bytes 3076
  1805.2 21.3 %copy-start.37 = (f32[256]{0:T(256)S(1)}, f32[256]{0:T(256)}, u32[]{:S(2)}) copy-start(f32[256]{0:T(256)} %get-tuple-element.12) | copy-start | bytes 3076
  1805.2 21.3 %copy-start.36 = (f32[1152]{0:T(1024)S(1)}, f32[1152]{0:T(1024)}, u32[]{:S(2)}) copy-start(f32[1152]{0:T(1024)} %get-tuple-element.17) | copy-start | bytes 13828
  1807.2 111.4 %all-gather.24.cloned.1.call-start = ((), (), s32[]{:S(2)}) async-start(), calls=%async_computation.13 | async-start | bytes 3481600 | tf_op jit(solution)/shard_map/all_gather | solution.py:245
  1808.2 10.1 collective-permute-start.9
  1826.5 20.1 %copy-start.12 = (f32[256,1152]{1,0:T(8,128)S(1)}, f32[256,1152]{1,0:T(8,128)}, u32[]{:S(2)}) copy-start(f32[256,1152]{1,0:T(8,128)} %get-tuple-element.48) | copy-start | bytes 3538948
  1835.9 11.9 copy-start.33
  1836.0 67.1 %collective-permute-start.8 = (f32[36,1152]{1,0:T(8,128)S(1)}, f32[36,1152]{1,0:T(8,128)S(1)}, u32[]{:S(2)}, u32[]{:S(2)}) collective-permute-start(f32[36,1152]{1,0:T(8,128)S(1)} %slice.59), channel_id=1, source_target_pairs={{0,8},{8,16},{16,24},{1,9},{9,17},{17,25},{2,10},{10,18},{18,26},{... | collective-permute-start | bytes 497672
  (14 other events, 20.0 us)
Sparse Core Ops, SparseCore 0:
  10.2 218.1 all-gather.13
  230.5 75.0 all-gather.15
  307.8 143.3 all-gather.17
  455.0 329.7 reduce-scatter.23
  786.9 143.8 all-gather.19
  933.0 87.3 all-reduce.10
  1024.0 104.5 reduce-scatter.19
  1132.4 267.9 reduce-scatter.17
  1404.4 330.6 reduce-scatter.21
  1738.2 61.7 reduce-scatter.25
  1801.5 25.4 all-gather.25
  1828.5 26.1 all-gather.21
  1856.2 27.3 all-gather.23
